TPU v7x, 256 devices: a whole 4x4x8 slice. The times are simulated.
256 devices in a mesh: edge: 64 (over y, z, x_lo), chan: 4 (over x_hi, core).
Axes of the slice: x: 4 (x_hi: 2, x_lo: 2; x = x_hi * 2 + x_lo), y: 4, z: 8, core: 2. Of those that a mesh axis runs over, the one named last changes fastest.
Arguments:
- node_states: bfloat16 [1024, 49, 256], P('edge', None, 'chan'), may hold values from -6 to 6
- edge_vectors: float32 [3, 32768], P(None, ('edge', 'chan')), may hold values from -5.6 to 5.6, as said below
- source_part: int32 [32768, 1], P('edge'), may hold values from 0 to 63; in each aligned block of 512 rows (0 to 511, 512 to 1023, ...) at most 16 rows name the same one
- source_slot: int32 [32768], P('edge'), may hold values from 0 to 15
- target_slot: int32 [32768], P('edge'), may hold values from 0 to 15
- live_edges: int32 [64], P('edge'), may hold values from 1 to 512, 24576 in all
- weight_zero: bfloat16 [7, 256, 7, 256], P(None, 'chan'), may hold values from -0.125 to 0.125
- weight_one: bfloat16 [2, 6, 256, 6, 256], P(None, None, 'chan'), may hold values from -0.109375 to 0.109375
- weight_two: bfloat16 [2, 5, 256, 5, 256], P(None, None, 'chan'), may hold values from -0.125 to 0.125
Outputs:
- aggregated: bfloat16 [1024, 49, 256], P('edge', None, 'chan')
Inputs may be any that keep to these rules, and one draw needn't show every extreme that they name: `source_part`: in each aligned block of 512 rows (the edges of one partition's slab) no partition number appears more than 16 times, and some number appears exactly 16 times. Edges are grouped by destination partition: the destination of an edge in slab p is node p * 16 + target_slot. `live_edges`: live slots stand at the front of each slab; the fullest slab is full. `edge_vectors`: every column has length between 0.8 and 5.6.
All inputs are finite; a program needn't handle non-finite values. No bound on the sum of `live_edges` on one device may be relied on, other than what follows from the above.
Results may differ from a plain program's by a relative error of at most 0.015.
Values may be sent and summed in bfloat16 or wider, within the bound.
A program may use at most 128 MiB of HBM per device.

v0:
```python
import math
import jax
import jax.numpy as jnp
import numpy as np
from jax import lax
from jax.sharding import PartitionSpec as P

LMAX = 6
MMAX = 2
cutoff_radius = 6.0
highest = lax.Precision.HIGHEST


def harmonics(coord_x, coord_y, coord_z, degree_top, order_top):
    results = {}
    real_part = [coord_x * 0.0 + 1.0]
    imag_part = [coord_x * 0.0]
    for azimuthal in range(1, order_top + 1):
        new_real = coord_x * real_part[-1] - coord_y * imag_part[-1]
        new_imag = coord_x * imag_part[-1] + coord_y * real_part[-1]
        real_part.append(new_real)
        imag_part.append(new_imag)
    for azimuthal in range(order_top + 1):
        start_value = (-1.0) ** azimuthal * math.prod(range(2 * azimuthal - 1, 0, -2))
        legendre = {azimuthal: coord_z * 0.0 + start_value}
        if azimuthal + 1 <= degree_top:
            legendre[azimuthal + 1] = coord_z * ((2 * azimuthal + 1) * start_value)
        for degree in range(azimuthal + 2, degree_top + 1):
            legendre[degree] = (
                (2 * degree - 1) * coord_z * legendre[degree - 1]
                - (degree + azimuthal - 1) * legendre[degree - 2]
            ) / (degree - azimuthal)
        for degree in range(azimuthal, degree_top + 1):
            factor = math.sqrt(
                (2 * degree + 1)
                / (4.0 * math.pi)
                * math.factorial(degree - azimuthal)
                / math.factorial(degree + azimuthal)
            )
            if azimuthal == 0:
                results[degree, 0] = factor * legendre[degree]
            else:
                results[degree, azimuthal] = (
                    math.sqrt(2.0) * factor * legendre[degree] * real_part[azimuthal]
                )
                results[degree, -azimuthal] = (
                    math.sqrt(2.0) * factor * legendre[degree] * imag_part[azimuthal]
                )
    return results


def kept_rows():
    row_list = [(degree, 0) for degree in range(LMAX + 1)]
    for azimuthal in range(1, MMAX + 1):
        row_list += [(degree, azimuthal) for degree in range(azimuthal, LMAX + 1)]
        row_list += [(degree, -azimuthal) for degree in range(azimuthal, LMAX + 1)]
    return row_list


def row_offsets():
    listing = []
    offset = 0
    for degree, azimuthal in kept_rows():
        listing.append((degree, offset))
        offset += 2 * degree + 1
    return listing


def invert_small(matrix):
    order_size = matrix.shape[0]
    work = np.concatenate([matrix, np.eye(order_size)], axis=1)
    for column in range(order_size):
        work[column] = work[column] / work[column, column]
        for row_index in range(order_size):
            if row_index != column:
                work[row_index] = work[row_index] - work[row_index, column] * work[column]
    return work[:, order_size:]


def sample_tables():
    sample_count = 2 * (LMAX + 1) ** 2
    positions = np.arange(sample_count) + 0.5
    height = 1.0 - 2.0 * positions / sample_count
    radius = np.sqrt(1.0 - height * height)
    azimuth = math.pi * (3.0 - math.sqrt(5.0)) * positions
    points = np.stack([radius * np.cos(azimuth), radius * np.sin(azimuth), height])
    values = harmonics(points[0], points[1], points[2], LMAX, LMAX)
    inverses = []
    for degree in range(LMAX + 1):
        sampled = np.stack([values[degree, azimuthal] for azimuthal in range(-degree, degree + 1)])
        inverses.append(sampled.T @ invert_small(sampled @ sampled.T))
    return (points, inverses)


def wigner_rows(vectors):
    length = jnp.sqrt(jnp.sum(vectors * vectors, axis=0))
    direction = vectors / length
    pick_first = jnp.where(jnp.abs(direction[0]) < 0.6, 1.0, 0.0).astype(jnp.float32)
    helper = jnp.stack([pick_first, 1.0 - pick_first, jnp.zeros_like(pick_first)])
    first_axis = jnp.cross(direction, helper, axis=0)
    first_axis = first_axis / jnp.sqrt(jnp.sum(first_axis * first_axis, axis=0))
    second_axis = jnp.cross(direction, first_axis, axis=0)
    frames = jnp.stack([first_axis, second_axis, direction])
    points, inverses = sample_tables()
    sample = jnp.asarray(points, jnp.float32)
    turned = jnp.einsum("rce,ck->rek", frames, sample, precision=highest)
    values = harmonics(turned[0], turned[1], turned[2], LMAX, MMAX)
    pieces = []
    for degree, azimuthal in kept_rows():
        table = jnp.asarray(inverses[degree], jnp.float32)
        pieces.append(jnp.dot(values[degree, azimuthal], table, precision=highest))
    compact = jnp.concatenate(pieces, axis=1)
    envelope = 0.5 * (jnp.cos(math.pi * length / cutoff_radius) + 1.0)
    return (compact, envelope)


def rotate_forward(compact_t, sources):
    rows_out = []
    for degree, offset in row_offsets():
        total = compact_t[offset].astype(jnp.float32)[None, :] * sources[degree * degree].astype(
            jnp.float32
        )
        for inner in range(1, 2 * degree + 1):
            total = total + compact_t[offset + inner].astype(jnp.float32)[None, :] * sources[
                degree * degree + inner
            ].astype(jnp.float32)
        rows_out.append(total)
    return jnp.stack(rows_out, axis=0).astype(jnp.bfloat16)


def rotate_back(compact_t, scaled):
    listing = row_offsets()
    coefs_out = []
    for degree in range(LMAX + 1):
        for inner in range(2 * degree + 1):
            total = None
            for row_index, (row_degree, offset) in enumerate(listing):
                if row_degree == degree:
                    term = compact_t[offset + inner].astype(jnp.float32)[None, :] * scaled[
                        :, row_index
                    ].astype(jnp.float32)
                    total = term if total is None else total + term
            coefs_out.append(total)
    return jnp.stack(coefs_out, axis=0).astype(jnp.bfloat16)


def convolve(turned, weight_zero, weight_one, weight_two, contract):
    end_zero = LMAX + 1
    end_one_plus = end_zero + LMAX
    end_one_minus = end_one_plus + LMAX
    end_two_plus = end_one_minus + LMAX - 1
    zero_part = turned[:end_zero]
    one_plus = turned[end_zero:end_one_plus]
    one_minus = turned[end_one_plus:end_one_minus]
    two_plus = turned[end_one_minus:end_two_plus]
    two_minus = turned[end_two_plus:]
    pattern = "lce,lcjd->dje"
    out_zero = contract(pattern, zero_part, weight_zero)
    out_one_plus = contract(pattern, one_plus, weight_one[0]) - contract(
        pattern, one_minus, weight_one[1]
    )
    out_one_minus = contract(pattern, one_minus, weight_one[0]) + contract(
        pattern, one_plus, weight_one[1]
    )
    out_two_plus = contract(pattern, two_plus, weight_two[0]) - contract(
        pattern, two_minus, weight_two[1]
    )
    out_two_minus = contract(pattern, two_minus, weight_two[0]) + contract(
        pattern, two_plus, weight_two[1]
    )
    return jnp.concatenate(
        [out_zero, out_one_plus, out_one_minus, out_two_plus, out_two_minus], axis=1
    )


def mixed_contract(pattern, first_operand, second_operand):
    return jnp.einsum(pattern, first_operand, second_operand, preferred_element_type=jnp.float32)


def one_hot(indices, width):
    return (indices[:, None] == jnp.arange(width, dtype=jnp.int32)[None, :]).astype(jnp.bfloat16)


def pick_columns(table, selector):
    picked = lax.dot_general(
        table, selector, (((0,), (1,)), ((), ())), preferred_element_type=jnp.float32
    )
    return picked.astype(jnp.bfloat16)


def pick_rows(selector, table):
    return jnp.dot(selector, table, preferred_element_type=jnp.float32).astype(jnp.bfloat16)


def shards(
    node_states,
    edge_vectors,
    source_part,
    source_slot,
    target_slot,
    live_edges,
    weight_zero,
    weight_one,
    weight_two,
):
    slab_size = source_slot.shape[0]
    local_nodes = node_states.shape[0]
    local_channels = node_states.shape[2]
    coef_count = node_states.shape[1]
    group_count = lax.axis_size("edge")
    capacity = max(2, 2 * slab_size // group_count)
    slot_total = group_count * capacity
    quarter, quarter_fade = wigner_rows(edge_vectors)
    compact, envelope = (
        lax.all_gather(quarter.astype(jnp.bfloat16), "chan", axis=0, tiled=True),
        lax.all_gather(quarter_fade.astype(jnp.bfloat16), "chan", axis=0, tiled=True),
    )
    compact_t = compact.T
    node_flat = node_states.reshape(local_nodes, coef_count * local_channels)
    owner_part = source_part[:, 0]
    owners = jnp.arange(group_count, dtype=jnp.int32)
    member = (owner_part[:, None] == owners[None, :]).astype(jnp.int32)
    earlier = jnp.cumsum(member, axis=0) - member
    position = jnp.sum(earlier * member, axis=1)
    slot_flat = owner_part * capacity + position
    requests = (
        jnp.zeros((slot_total,), jnp.int32)
        .at[slot_flat]
        .set(source_slot)
        .reshape(group_count, capacity)
    )
    slot_select = one_hot(slot_flat, slot_total)
    wanted = lax.all_to_all(requests, "edge", split_axis=0, concat_axis=0, tiled=True)
    picked = pick_rows(one_hot(wanted.reshape(-1), local_nodes), node_flat)
    returned = lax.all_to_all(
        picked.reshape(group_count, capacity, coef_count * local_channels),
        "edge",
        split_axis=0,
        concat_axis=0,
        tiled=True,
    )
    sources = pick_columns(
        returned.reshape(slot_total, coef_count * local_channels), slot_select
    ).reshape(coef_count, local_channels, slab_size)
    turned = rotate_forward(compact_t, sources)
    channel_mix = lax.psum_scatter(
        convolve(turned, weight_zero, weight_one, weight_two, mixed_contract).astype(jnp.bfloat16),
        "chan",
        scatter_dimension=0,
        tiled=True,
    ).astype(jnp.float32)
    alive_mask = (jnp.arange(slab_size, dtype=jnp.int32) < live_edges[0]).astype(jnp.float32)
    scaling = envelope.astype(jnp.float32) * alive_mask
    scaled = (channel_mix * scaling).astype(jnp.bfloat16)
    message = rotate_back(compact_t, scaled).reshape(coef_count * local_channels, slab_size)
    selector = (jnp.arange(local_nodes, dtype=jnp.int32)[:, None] == target_slot[None, :]).astype(
        jnp.bfloat16
    )
    summed = lax.dot_general(
        selector, message, (((1,), (1,)), ((), ())), preferred_element_type=jnp.float32
    )
    return summed.astype(jnp.bfloat16).reshape(local_nodes, coef_count, local_channels)


def solution(mesh):
    in_specs = (
        P("edge", None, "chan"),
        P(None, ("edge", "chan")),
        P("edge", None),
        P("edge"),
        P("edge"),
        P("edge"),
        P(None, "chan", None, None),
        P(None, None, "chan", None, None),
        P(None, None, "chan", None, None),
    )
    out_specs = P("edge", None, "chan")
    return jax.shard_map(shards, mesh=mesh, in_specs=in_specs, out_specs=out_specs, check_vma=False)
```

profile of v0, /device:TPU:1, one launch (start us, length us, event | category | flops | bytes accessed | tf_op | source)
XLA Modules:
  0.0 345.9 jit_solution(5656310908398579439)
XLA Ops:
  6.5 0.8 fusion.497
  7.4 1.2 reduce-window.6
  8.8 0.8 fusion.490
  9.6 1.3 compare_select_fusion
  10.9 2.6 scatter_custom_fusion
  13.5 0.7 all_to_all.9
  14.2 13.6 %all-to-all-start = ((s32[64,1,16]{2,1,0:T(1,128)}), s32[64,1,16]{2,1,0:T(1,128)S(1)}, u32[]{:S(2)}, u32[]{:S(2)}) async-start(s32[64,1,16]{2,1,0:T(1,128)} %bitcast.27), calls=%async_computation | async-start | bytes 65536 | tf_op jit(solution)/shard_map/all_to_all | solution.py:233
  27.8 0.7 multiply_reduce_fusion.1
  28.5 1.0 copy.58
  29.7 7.3 %all-to-all-done = s32[64,1,16]{2,1,0:T(1,128)S(1)} async-done(((s32[64,1,16]{2,1,0:T(1,128)}), s32[64,1,16]{2,1,0:T(1,128)S(1)}, u32[]{:S(2)}, u32[]{:S(2)}) %all-to-all-start) | async-done | bytes 4128 | tf_op jit(solution)/shard_map/all_to_all | solution.py:233
  37.5 0.7 reduce.5
  38.3 4.7 %convolution_convert_fusion = bf16[1024,3136]{0,1:T(8,128)(2,1)} fusion(bf16[16,3136]{1,0:T(8,128)(2,1)S(1)} %reshape.10748, s32[1024]{0:T(1024)S(1)} %eq.79), kind=kOutput, calls=%fused_computation.1 | convolution fusion | flops 105988096 | bytes 6526976 | tf_op jit(solution)/shard_map/dot_general | solution.py:192
  42.9 9.3 %copy.59 = bf16[1024,3136]{1,0:T(8,128)(2,1)} copy(bf16[1024,3136]{0,1:T(8,128)(2,1)} %convolution_convert_fusion) | data formatting | bytes 12845056 | tf_op jit(solution)/shard_map/convert_element_type | solution.py:192
  52.3 5.8 %all-to-all-start.1 = ((bf16[64,16,3136]{2,1,0:T(8,128)(2,1)}), bf16[64,16,3136]{2,1,0:T(8,128)(2,1)}, u32[]{:S(2)}, u32[]{:S(2)}) async-start(bf16[64,16,3136]{2,1,0:T(8,128)(2,1)} %bitcast.1286), calls=%async_computation.1 | async-start | bytes 13107200 | tf_op jit(solution)/shard_map/all_to_all | solution.py:235
  66.5 2.1 concatenate.16
  68.6 9.9 %all_gather.6 = bf16[512,235]{0,1:T(8,128)(2,1)S(1)} all-gather(bf16[128,235]{0,1:T(8,128)(2,1)S(1)} %concatenate.16), channel_id=1, replica_groups=mesh['edge'=64,'chan'=4] {'chan'}, dimensions={0}, use_global_device_ids=true | all-gather | bytes 300800 | tf_op jit(solution)/shard_map/all_gather | solution.py:215
  78.5 0.7 slice_convert_fusion.225
  80.4 0.6 slice_convert_fusion.129
  81.0 0.7 slice_convert_fusion.23
  81.7 0.7 slice_convert_fusion.209
  83.0 0.7 slice_convert_fusion.170
  83.6 0.6 slice_convert_fusion.150
  84.3 0.7 slice_convert_fusion.113
  84.9 0.7 slice_convert_fusion.57
  85.6 0.7 slice_convert_fusion.12
  86.3 1.3 fusion.803
  87.6 1.2 fusion.802
  88.8 113.9 %all-to-all-done.1 = bf16[64,16,3136]{2,1,0:T(8,128)(2,1)} async-done(((bf16[64,16,3136]{2,1,0:T(8,128)(2,1)}), bf16[64,16,3136]{2,1,0:T(8,128)(2,1)}, u32[]{:S(2)}, u32[]{:S(2)}) %all-to-all-start.1) | async-done | bytes 6422560 | tf_op jit(solution)/shard_map/all_to_all | solution.py:235
  203.0 7.0 %convolution_convert_fusion.1 = bf16[3136,512]{1,0:T(8,128)(2,1)S(1)} fusion(bf16[1024,3136]{1,0:T(8,128)(2,1)} %bitcast.29, s32[512]{0:T(512)} %bitcast.1775), kind=kOutput, calls=%fused_computation.2 | convolution fusion | flops 3290464256 | bytes 9635840 | tf_op jit(solution)/shard_map/dot_general | solution.py:185
  210.3 0.9 constant_dynamic-update-slice_fusion.17
  211.2 0.8 constant_dynamic-update-slice_fusion.11
  212.0 0.8 constant_dynamic-update-slice_fusion.10
  213.7 1.0 fusion.12
  215.9 1.0 fusion.11
  217.5 0.8 constant_dynamic-update-slice_fusion.21
  219.0 0.9 fusion.14
  220.8 0.9 fusion.13
  222.6 2.5 bitcast_dynamic-update-slice_fusion
  225.0 2.2 bitcast_dynamic-update-slice_fusion.2
  227.3 2.2 bitcast_dynamic-update-slice_fusion.1
  229.4 2.0 fusion.5
  231.4 1.9 fusion.7
  233.4 14.5 %copy.65 = bf16[256,29,512]{2,1,0:T(8,128)(2,1)} copy(bf16[256,29,512]{0,2,1:T(8,128)(2,1)} %fusion.7) | data formatting | bytes 15204352 | tf_op jit(solution)/shard_map/concatenate | solution.py:171
  248.5 9.3 %all-gather = bf16[4,1,128]{2,1,0:T(2,128)(2,1)S(1)} all-gather(bf16[1,1,128]{2,1,0:T(2,128)(2,1)S(1)} %copy-done.205), channel_id=1, replica_groups=mesh['edge'=64,'chan'=4] {'chan'}, dimensions={0}, use_global_device_ids=true | all-gather | bytes 1280 | tf_op jit(solution)/shard_map/all_gather | solution.py:216
  258.6 71.5 %reduce-scatter.2.cloned.1.call-done = bf16[64,29,512]{2,1,0:T(8,128)(2,1)} async-done(((bf16[256,29,512]{2,1,0:T(8,128)(2,1)}), bf16[64,29,512]{2,1,0:T(8,128)(2,1)}) %reduce-scatter.2.cloned.1.call-update) | async-done | bytes 1900560 | tf_op jit(solution)/shard_map/reduce_scatter | solution.py:246
  330.1 2.7 multiply_convert_fusion
  337.2 0.9 convolution_convert_fusion.2
  338.3 0.7 copy.67
  (550 shorter events, 18.9 us)
Async XLA Ops:
  6.5 216.0 %copy-start = (bf16[7,64,7,256]{3,1,2,0:T(8,128)(2,1)S(1)}, bf16[7,64,7,256]{3,1,2,0:T(8,128)(2,1)}, u32[]{:S(2)}) copy-start(bf16[7,64,7,256]{3,1,2,0:T(8,128)(2,1)} %param.47) | copy-start | bytes 4816900
  14.2 22.7 %all-to-all-start = ((s32[64,1,16]{2,1,0:T(1,128)}), s32[64,1,16]{2,1,0:T(1,128)S(1)}, u32[]{:S(2)}, u32[]{:S(2)}) async-start(s32[64,1,16]{2,1,0:T(1,128)} %bitcast.27), calls=%async_computation | async-start | bytes 65536 | tf_op jit(solution)/shard_map/all_to_all | solution.py:233
  52.3 150.4 %all-to-all-start.1 = ((bf16[64,16,3136]{2,1,0:T(8,128)(2,1)}), bf16[64,16,3136]{2,1,0:T(8,128)(2,1)}, u32[]{:S(2)}, u32[]{:S(2)}) async-start(bf16[64,16,3136]{2,1,0:T(8,128)(2,1)} %bitcast.1286), calls=%async_computation.1 | async-start | bytes 13107200 | tf_op jit(solution)/shard_map/all_to_all | solution.py:235
  58.1 272.0 %reduce-scatter.2.cloned.1.call-start = ((), (), s32[]{:S(2)}) async-start(), calls=%async_computation.3 | async-start | bytes 10485760 | tf_op jit(solution)/shard_map/reduce_scatter | solution.py:246
  62.2 24.0 %copy-start.3 = (bf16[2,5,64,5,256]{4,2,3,1,0:T(8,128)(2,1)S(1)}, bf16[2,5,64,5,256]{4,2,3,1,0:T(8,128)(2,1)}, u32[]{:S(2)}) copy-start(bf16[2,5,64,5,256]{4,2,3,1,0:T(8,128)(2,1)} %param.49) | copy-start | bytes 4915204
  68.5 19.0 %copy-start.2 = (bf16[2,6,64,6,256]{4,2,3,1,0:T(8,128)(2,1)S(1)}, bf16[2,6,64,6,256]{4,2,3,1,0:T(8,128)(2,1)}, u32[]{:S(2)}) copy-start(bf16[2,6,64,6,256]{4,2,3,1,0:T(8,128)(2,1)} %param.48) | copy-start | bytes 7077892
  202.8 9.2 %copy-start.159 = (f32[1,512]{1,0:T(1,128)S(1)}, f32[1,512]{1,0:T(1,128)}, u32[]{:S(2)}) copy-start(f32[1,512]{1,0:T(1,128)} %get-tuple-element.196) | copy-start | bytes 6148
  202.8 9.2 %copy-start.167 = (f32[1,512]{1,0:T(1,128)S(1)}, f32[1,512]{1,0:T(1,128)}, u32[]{:S(2)}) copy-start(f32[1,512]{1,0:T(1,128)} %get-tuple-element.197) | copy-start | bytes 6148
  202.8 9.2 %copy-start.172 = (f32[1,512]{1,0:T(1,128)S(1)}, f32[1,512]{1,0:T(1,128)}, u32[]{:S(2)}) copy-start(f32[1,512]{1,0:T(1,128)} %get-tuple-element.198) | copy-start | bytes 6148
  202.8 9.2 %copy-start.177 = (f32[1,512]{1,0:T(1,128)S(1)}, f32[1,512]{1,0:T(1,128)}, u32[]{:S(2)}) copy-start(f32[1,512]{1,0:T(1,128)} %get-tuple-element.199) | copy-start | bytes 6148
  202.8 10.0 %copy-start.93 = (f32[1,512]{1,0:T(1,128)S(1)}, f32[1,512]{1,0:T(1,128)}, u32[]{:S(2)}) copy-start(f32[1,512]{1,0:T(1,128)} %get-tuple-element.187) | copy-start | bytes 6148
  202.8 10.0 %copy-start.103 = (f32[1,512]{1,0:T(1,128)S(1)}, f32[1,512]{1,0:T(1,128)}, u32[]{:S(2)}) copy-start(f32[1,512]{1,0:T(1,128)} %get-tuple-element.188) | copy-start | bytes 6148
  202.8 10.0 %copy-start.110 = (f32[1,512]{1,0:T(1,128)S(1)}, f32[1,512]{1,0:T(1,128)}, u32[]{:S(2)}) copy-start(f32[1,512]{1,0:T(1,128)} %get-tuple-element.190) | copy-start | bytes 6148
  202.8 10.0 %copy-start.116 = (f32[1,512]{1,0:T(1,128)S(1)}, f32[1,512]{1,0:T(1,128)}, u32[]{:S(2)}) copy-start(f32[1,512]{1,0:T(1,128)} %get-tuple-element.191) | copy-start | bytes 6148
  202.8 10.0 %copy-start.121 = (f32[1,512]{1,0:T(1,128)S(1)}, f32[1,512]{1,0:T(1,128)}, u32[]{:S(2)}) copy-start(f32[1,512]{1,0:T(1,128)} %get-tuple-element.192) | copy-start | bytes 6148
  202.9 10.0 %copy-start.127 = (f32[1,512]{1,0:T(1,128)S(1)}, f32[1,512]{1,0:T(1,128)}, u32[]{:S(2)}) copy-start(f32[1,512]{1,0:T(1,128)} %get-tuple-element.193) | copy-start | bytes 6148
  202.9 10.0 %copy-start.135 = (f32[1,512]{1,0:T(1,128)S(1)}, f32[1,512]{1,0:T(1,128)}, u32[]{:S(2)}) copy-start(f32[1,512]{1,0:T(1,128)} %get-tuple-element.194) | copy-start | bytes 6148
  202.9 10.0 %copy-start.141 = (f32[1,512]{1,0:T(1,128)S(1)}, f32[1,512]{1,0:T(1,128)}, u32[]{:S(2)}) copy-start(f32[1,512]{1,0:T(1,128)} %get-tuple-element.195) | copy-start | bytes 6148
  202.9 10.0 %copy-start.149 = (f32[1,512]{1,0:T(1,128)S(1)}, f32[1,512]{1,0:T(1,128)}, u32[]{:S(2)}) copy-start(f32[1,512]{1,0:T(1,128)} %get-tuple-element.189) | copy-start | bytes 6148
  202.9 10.1 %copy-start.12 = (f32[1,512]{1,0:T(1,128)S(1)}, f32[1,512]{1,0:T(1,128)}, u32[]{:S(2)}) copy-start(f32[1,512]{1,0:T(1,128)} %get-tuple-element.176) | copy-start | bytes 6148
  202.9 10.1 %copy-start.18 = (f32[1,512]{1,0:T(1,128)S(1)}, f32[1,512]{1,0:T(1,128)}, u32[]{:S(2)}) copy-start(f32[1,512]{1,0:T(1,128)} %get-tuple-element.177) | copy-start | bytes 6148
  202.9 10.1 %copy-start.25 = (f32[1,512]{1,0:T(1,128)S(1)}, f32[1,512]{1,0:T(1,128)}, u32[]{:S(2)}) copy-start(f32[1,512]{1,0:T(1,128)} %get-tuple-element.178) | copy-start | bytes 6148
  202.9 10.1 %copy-start.31 = (f32[1,512]{1,0:T(1,128)S(1)}, f32[1,512]{1,0:T(1,128)}, u32[]{:S(2)}) copy-start(f32[1,512]{1,0:T(1,128)} %get-tuple-element.179) | copy-start | bytes 6148
  202.9 10.1 %copy-start.37 = (f32[1,512]{1,0:T(1,128)S(1)}, f32[1,512]{1,0:T(1,128)}, u32[]{:S(2)}) copy-start(f32[1,512]{1,0:T(1,128)} %get-tuple-element.180) | copy-start | bytes 6148
  202.9 10.1 %copy-start.43 = (f32[1,512]{1,0:T(1,128)S(1)}, f32[1,512]{1,0:T(1,128)}, u32[]{:S(2)}) copy-start(f32[1,512]{1,0:T(1,128)} %get-tuple-element.181) | copy-start | bytes 6148
  203.0 10.1 %copy-start.49 = (f32[1,512]{1,0:T(1,128)S(1)}, f32[1,512]{1,0:T(1,128)}, u32[]{:S(2)}) copy-start(f32[1,512]{1,0:T(1,128)} %get-tuple-element.182) | copy-start | bytes 6148
  203.0 10.1 %copy-start.56 = (f32[1,512]{1,0:T(1,128)S(1)}, f32[1,512]{1,0:T(1,128)}, u32[]{:S(2)}) copy-start(f32[1,512]{1,0:T(1,128)} %get-tuple-element.183) | copy-start | bytes 6148
  203.0 10.1 %copy-start.63 = (f32[1,512]{1,0:T(1,128)S(1)}, f32[1,512]{1,0:T(1,128)}, u32[]{:S(2)}) copy-start(f32[1,512]{1,0:T(1,128)} %get-tuple-element.184) | copy-start | bytes 6148
  203.0 10.1 %copy-start.71 = (f32[1,512]{1,0:T(1,128)S(1)}, f32[1,512]{1,0:T(1,128)}, u32[]{:S(2)}) copy-start(f32[1,512]{1,0:T(1,128)} %get-tuple-element.185) | copy-start | bytes 6148
  203.0 10.1 %copy-start.82 = (f32[1,512]{1,0:T(1,128)S(1)}, f32[1,512]{1,0:T(1,128)}, u32[]{:S(2)}) copy-start(f32[1,512]{1,0:T(1,128)} %get-tuple-element.186) | copy-start | bytes 6148
  247.9 85.1 %copy-start.164 = (f32[1,512]{1,0:T(1,128)S(1)}, f32[1,512]{1,0:T(1,128)}, u32[]{:S(2)}) copy-start(f32[1,512]{1,0:T(1,128)} %get-tuple-element.162) | copy-start | bytes 6148
  247.9 85.1 %copy-start.201 = (f32[1,512]{1,0:T(1,128)S(1)}, f32[1,512]{1,0:T(1,128)}, u32[]{:S(2)}) copy-start(f32[1,512]{1,0:T(1,128)} %get-tuple-element.208) | copy-start | bytes 6148
  247.9 85.2 %copy-start.158 = (f32[1,512]{1,0:T(1,128)S(1)}, f32[1,512]{1,0:T(1,128)}, u32[]{:S(2)}) copy-start(f32[1,512]{1,0:T(1,128)} %get-tuple-element.161) | copy-start | bytes 6148
  247.9 85.2 %copy-start.199 = (f32[1,512]{1,0:T(1,128)S(1)}, f32[1,512]{1,0:T(1,128)}, u32[]{:S(2)}) copy-start(f32[1,512]{1,0:T(1,128)} %get-tuple-element.210) | copy-start | bytes 6148
  247.9 85.2 %copy-start.152 = (f32[1,512]{1,0:T(1,128)S(1)}, f32[1,512]{1,0:T(1,128)}, u32[]{:S(2)}) copy-start(f32[1,512]{1,0:T(1,128)} %get-tuple-element.160) | copy-start | bytes 6148
  247.9 85.2 %copy-start.198 = (f32[1,512]{1,0:T(1,128)S(1)}, f32[1,512]{1,0:T(1,128)}, u32[]{:S(2)}) copy-start(f32[1,512]{1,0:T(1,128)} %get-tuple-element.209) | copy-start | bytes 6148
  247.9 85.3 %copy-start.144 = (f32[1,512]{1,0:T(1,128)S(1)}, f32[1,512]{1,0:T(1,128)}, u32[]{:S(2)}) copy-start(f32[1,512]{1,0:T(1,128)} %get-tuple-element.159) | copy-start | bytes 6148
  248.0 85.3 %copy-start.202 = (f32[1,512]{1,0:T(1,128)S(1)}, f32[1,512]{1,0:T(1,128)}, u32[]{:S(2)}) copy-start(f32[1,512]{1,0:T(1,128)} %get-tuple-element.207) | copy-start | bytes 6148
  248.0 85.4 %copy-start.134 = (f32[1,512]{1,0:T(1,128)S(1)}, f32[1,512]{1,0:T(1,128)}, u32[]{:S(2)}) copy-start(f32[1,512]{1,0:T(1,128)} %get-tuple-element.158) | copy-start | bytes 6148
  248.0 85.4 %copy-start.200 = (f32[1,512]{1,0:T(1,128)S(1)}, f32[1,512]{1,0:T(1,128)}, u32[]{:S(2)}) copy-start(f32[1,512]{1,0:T(1,128)} %get-tuple-element.206) | copy-start | bytes 6148
  248.0 85.5 %copy-start.126 = (f32[1,512]{1,0:T(1,128)S(1)}, f32[1,512]{1,0:T(1,128)}, u32[]{:S(2)}) copy-start(f32[1,512]{1,0:T(1,128)} %get-tuple-element.157) | copy-start | bytes 6148
  248.0 85.5 %copy-start.197 = (f32[1,512]{1,0:T(1,128)S(1)}, f32[1,512]{1,0:T(1,128)}, u32[]{:S(2)}) copy-start(f32[1,512]{1,0:T(1,128)} %get-tuple-element.205) | copy-start | bytes 6148
  248.0 85.6 %copy-start.196 = (f32[1,512]{1,0:T(1,128)S(1)}, f32[1,512]{1,0:T(1,128)}, u32[]{:S(2)}) copy-start(f32[1,512]{1,0:T(1,128)} %get-tuple-element.204) | copy-start | bytes 6148
  258.5 75.2 %copy-start.193 = (f32[1,512]{1,0:T(1,128)S(1)}, f32[1,512]{1,0:T(1,128)}, u32[]{:S(2)}) copy-start(f32[1,512]{1,0:T(1,128)} %get-tuple-element.203) | copy-start | bytes 6148
  258.5 75.3 %copy-start.190 = (f32[1,512]{1,0:T(1,128)S(1)}, f32[1,512]{1,0:T(1,128)}, u32[]{:S(2)}) copy-start(f32[1,512]{1,0:T(1,128)} %get-tuple-element.202) | copy-start | bytes 6148
  258.5 75.4 %copy-start.187 = (f32[1,512]{1,0:T(1,128)S(1)}, f32[1,512]{1,0:T(1,128)}, u32[]{:S(2)}) copy-start(f32[1,512]{1,0:T(1,128)} %get-tuple-element.201) | copy-start | bytes 6148
  258.5 75.4 %copy-start.183 = (f32[1,512]{1,0:T(1,128)S(1)}, f32[1,512]{1,0:T(1,128)}, u32[]{:S(2)}) copy-start(f32[1,512]{1,0:T(1,128)} %get-tuple-element.200) | copy-start | bytes 6148
  258.6 75.5 %copy-start.178 = (f32[1,512]{1,0:T(1,128)S(1)}, f32[1,512]{1,0:T(1,128)}, u32[]{:S(2)}) copy-start(f32[1,512]{1,0:T(1,128)} %get-tuple-element.199) | copy-start | bytes 6148
  (165 other events, 385.6 us)
Sparse Core Ops, SparseCore 0:
  248.0 82.0 reduce-scatter.1
where the time goes:
time: 347 us; the launch traced here: 346 us
  waiting for transfers between devices  193 us (56%)
  local copies, waits for them, and re-layouts  35.9 us (10%)
  matrix products  34.4 us (10%)
  other arithmetic  26.4 us (8%)
  starting transfers between devices  19.5 us (6%)
  blocking collectives  19.2 us (6%)
  between operations  17.8 us (5%)
    all_to_all x1, waiting for transfers between devices, shards(): lax.all_to_all(picked.reshape(group_count, capacity, coef_count * local_c...  114 us
    reduce_scatter x1, waiting for transfers between devices, shards(): lax.psum_scatter(convolve(turned, weight_zero, weight_one, weight_two, mi...  71.5 us
    dot_general x9, matrix products, mixed_contract(): jnp.einsum(pattern, first_operand, second_operand, preferred_element_type...  14.5 us
    concatenate x1, local copies, waits for them, and re-layouts, convolve(): jnp.concatenate([out_zero, out_one_plus, out_one_minus, out_two_plus, out...  14.5 us
    all_to_all x1, starting transfers between devices, shards(): lax.all_to_all(requests, 'edge', split_axis=0, concat_axis=0, tiled=True)  13.6 us
    all_gather x1, blocking collectives, shards(): lax.all_gather(quarter.astype(jnp.bfloat16), 'chan', axis=0, tiled=True)  9.89 us
    all_gather x1, blocking collectives, shards(): lax.all_gather(quarter_fade.astype(jnp.bfloat16), 'chan', axis=0, tiled=T...  9.35 us
    convert_element_type x1, local copies, waits for them, and re-layouts, pick_rows(): jnp.dot(selector, table, preferred_element_type=jnp.float32)  9.26 us
  transfers between devices with their start and end apart: 3, of which 3 were waited for; matrix products, arithmetic and copies ran while one was open for 6% of the time, Pallas kernels for 0%

commit v1 on v0

--- a/solution.py
+++ b/solution.py
@@ -203,6 +203,13 @@
     weight_one,
     weight_two,
 ):
+
+    def _use_axis_part(sheet, a_name):
+        a_next = lax.axis_size(a_name)
+        z = jnp.stack(a_next * [sheet])
+        u1 = lax.all_to_all(z, a_name, 0, 0)
+        return jnp.concatenate(u1, axis=0)
+
     slab_size = source_slot.shape[0]
     local_nodes = node_states.shape[0]
     local_channels = node_states.shape[2]
@@ -213,7 +220,7 @@
     quarter, quarter_fade = wigner_rows(edge_vectors)
     compact, envelope = (
         lax.all_gather(quarter.astype(jnp.bfloat16), "chan", axis=0, tiled=True),
-        lax.all_gather(quarter_fade.astype(jnp.bfloat16), "chan", axis=0, tiled=True),
+        _use_axis_part(quarter_fade.astype(jnp.bfloat16), "chan"),
     )
     compact_t = compact.T
     node_flat = node_states.reshape(local_nodes, coef_count * local_channels)

time: 347 us -> 347 us (level)
  blocking collectives: 19.2 us -> 9.91 us
  starting transfers between devices: 19.5 us -> 26.4 us
    all_gather x1 -> x0, blocking collectives: 9.35 us -> none  [shards(): lax.all_gather(quarter_fade.astype(jnp.bfloat16), 'chan', axis=0, tiled=T...]
    all_to_all x0 -> x1, starting transfers between devices: none -> 6.96 us  [_use_axis_part(): u1 = lax.all_to_all(z, a_name, 0, 0)]
    all_to_all x0 -> x1, waiting for transfers between devices: none -> 3.87 us  [_use_axis_part(): u1 = lax.all_to_all(z, a_name, 0, 0)]
    unnamed x69 -> x68, other arithmetic: 9.1 us -> 8.5 us
  transfers between devices with their start and end apart: 3 -> 4, of which waited for: 3 -> 4; matrix products, arithmetic and copies ran while one was open for 6% -> 7% of each run, Pallas kernels for 0% -> 0%
where the time goes in v1:
time: 347 us; the launch traced here: 346 us
  waiting for transfers between devices  195 us (56%)
  local copies, waits for them, and re-layouts  36.2 us (10%)
  matrix products  34.4 us (10%)
  other arithmetic  26.4 us (8%)
  starting transfers between devices  26.4 us (8%)
  between operations  17.7 us (5%)
  blocking collectives  9.91 us (3%)
    all_to_all x1, waiting for transfers between devices, shards(): lax.all_to_all(picked.reshape(group_count, capacity, coef_count * local_c...  114 us
    reduce_scatter x1, waiting for transfers between devices, shards(): lax.psum_scatter(convolve(turned, weight_zero, weight_one, weight_two, mi...  69.5 us
    dot_general x9, matrix products, mixed_contract(): jnp.einsum(pattern, first_operand, second_operand, preferred_element_type...  14.5 us
    concatenate x1, local copies, waits for them, and re-layouts, convolve(): jnp.concatenate([out_zero, out_one_plus, out_one_minus, out_two_plus, out...  14.5 us
    all_to_all x1, starting transfers between devices, shards(): lax.all_to_all(requests, 'edge', split_axis=0, concat_axis=0, tiled=True)  13.6 us
    all_gather x1, blocking collectives, shards(): lax.all_gather(quarter.astype(jnp.bfloat16), 'chan', axis=0, tiled=True)  9.91 us
    convert_element_type x1, local copies, waits for them, and re-layouts, pick_rows(): jnp.dot(selector, table, preferred_element_type=jnp.float32)  9.05 us
    unnamed x68, other arithmetic  8.5 us
  transfers between devices with their start and end apart: 4, of which 4 were waited for; matrix products, arithmetic and copies ran while one was open for 7% of the time, Pallas kernels for 0%

profile of v1, /device:TPU:1, one launch (start us, length us, event | category | flops | bytes accessed | tf_op | source)
XLA Modules:
  0.0 345.7 jit_solution(17183697845819492272)
XLA Ops:
  6.5 0.8 fusion.497
  7.4 1.2 reduce-window.6
  8.8 0.8 fusion.490
  9.6 1.3 compare_select_fusion
  10.9 2.6 scatter_custom_fusion
  13.5 0.7 all_to_all.13
  14.2 13.6 %all-to-all-start = ((s32[64,1,16]{2,1,0:T(1,128)}), s32[64,1,16]{2,1,0:T(1,128)S(1)}, u32[]{:S(2)}, u32[]{:S(2)}) async-start(s32[64,1,16]{2,1,0:T(1,128)} %bitcast.27), calls=%async_computation | async-start | bytes 65536 | tf_op jit(solution)/shard_map/all_to_all | solution.py:240
  27.8 0.7 multiply_reduce_fusion.1
  28.5 1.0 copy.58
  29.7 7.3 %all-to-all-done = s32[64,1,16]{2,1,0:T(1,128)S(1)} async-done(((s32[64,1,16]{2,1,0:T(1,128)}), s32[64,1,16]{2,1,0:T(1,128)S(1)}, u32[]{:S(2)}, u32[]{:S(2)}) %all-to-all-start) | async-done | bytes 4128 | tf_op jit(solution)/shard_map/all_to_all | solution.py:240
  37.5 0.7 reduce.5
  38.3 4.7 %convolution_convert_fusion = bf16[1024,3136]{0,1:T(8,128)(2,1)} fusion(bf16[16,3136]{1,0:T(8,128)(2,1)S(1)} %reshape.10767, s32[1024]{0:T(1024)S(1)} %eq.79), kind=kOutput, calls=%fused_computation.1 | convolution fusion | flops 105988096 | bytes 6526976 | tf_op jit(solution)/shard_map/dot_general | solution.py:192
  43.0 9.1 %copy.59 = bf16[1024,3136]{1,0:T(8,128)(2,1)} copy(bf16[1024,3136]{0,1:T(8,128)(2,1)} %convolution_convert_fusion) | data formatting | bytes 12845056 | tf_op jit(solution)/shard_map/convert_element_type | solution.py:192
  52.1 5.9 %all-to-all-start.1 = ((bf16[64,16,3136]{2,1,0:T(8,128)(2,1)}), bf16[64,16,3136]{2,1,0:T(8,128)(2,1)}, u32[]{:S(2)}, u32[]{:S(2)}) async-start(bf16[64,16,3136]{2,1,0:T(8,128)(2,1)} %bitcast.1284), calls=%async_computation.1 | async-start | bytes 13107200 | tf_op jit(solution)/shard_map/all_to_all | solution.py:242
  66.3 2.1 concatenate.16
  68.3 9.9 %all_gather.3 = bf16[512,235]{0,1:T(8,128)(2,1)S(1)} all-gather(bf16[128,235]{0,1:T(8,128)(2,1)S(1)} %concatenate.16), channel_id=1, replica_groups=mesh['edge'=64,'chan'=4] {'chan'}, dimensions={0}, use_global_device_ids=true | all-gather | bytes 300800 | tf_op jit(solution)/shard_map/all_gather | solution.py:222
  78.3 0.7 slice_convert_fusion.225
  80.2 0.6 slice_convert_fusion.129
  80.8 0.7 slice_convert_fusion.23
  81.5 0.7 slice_convert_fusion.209
  82.8 0.7 slice_convert_fusion.170
  84.1 0.7 slice_convert_fusion.113
  84.8 0.7 slice_convert_fusion.57
  85.4 0.6 slice_convert_fusion.12
  86.1 1.3 fusion.803
  87.4 1.2 fusion.802
  88.6 113.9 %all-to-all-done.1 = bf16[64,16,3136]{2,1,0:T(8,128)(2,1)} async-done(((bf16[64,16,3136]{2,1,0:T(8,128)(2,1)}), bf16[64,16,3136]{2,1,0:T(8,128)(2,1)}, u32[]{:S(2)}, u32[]{:S(2)}) %all-to-all-start.1) | async-done | bytes 6422560 | tf_op jit(solution)/shard_map/all_to_all | solution.py:242
  202.8 7.0 %convolution_convert_fusion.1 = bf16[3136,512]{1,0:T(8,128)(2,1)S(1)} fusion(bf16[1024,3136]{1,0:T(8,128)(2,1)} %bitcast.29, s32[512]{0:T(512)} %bitcast.1773), kind=kOutput, calls=%fused_computation.2 | convolution fusion | flops 3290464256 | bytes 9635840 | tf_op jit(solution)/shard_map/dot_general | solution.py:185
  210.1 0.9 constant_dynamic-update-slice_fusion.17
  211.0 0.8 constant_dynamic-update-slice_fusion.11
  211.8 0.8 constant_dynamic-update-slice_fusion.10
  213.5 1.0 fusion.12
  215.7 1.0 fusion.11
  217.3 0.8 constant_dynamic-update-slice_fusion.21
  218.8 0.9 fusion.14
  220.6 0.9 fusion.13
  222.4 2.5 bitcast_dynamic-update-slice_fusion
  224.9 2.2 bitcast_dynamic-update-slice_fusion.2
  227.1 2.2 bitcast_dynamic-update-slice_fusion.1
  229.3 2.0 fusion.5
  231.2 1.9 fusion.7
  233.2 14.5 %copy.65 = bf16[256,29,512]{2,1,0:T(8,128)(2,1)} copy(bf16[256,29,512]{0,2,1:T(8,128)(2,1)} %fusion.7) | data formatting | bytes 15204352 | tf_op jit(solution)/shard_map/concatenate | solution.py:171
  248.9 7.0 %all-to-all-start.2 = ((bf16[4,1,128]{2,1,0:T(2,128)(2,1)}), bf16[4,1,128]{2,1,0:T(2,128)(2,1)S(1)}, u32[]{:S(2)}, u32[]{:S(2)}) async-start(bf16[4,1,128]{2,1,0:T(2,128)(2,1)} %stack.36), calls=%async_computation.3 | async-start | bytes 4096 | tf_op jit(solution)/shard_map/all_to_all | solution.py:210
  256.5 3.9 %all-to-all-done.2 = bf16[4,1,128]{2,1,0:T(2,128)(2,1)S(1)} async-done(((bf16[4,1,128]{2,1,0:T(2,128)(2,1)}), bf16[4,1,128]{2,1,0:T(2,128)(2,1)S(1)}, u32[]{:S(2)}, u32[]{:S(2)}) %all-to-all-start.2) | async-done | bytes 1056 | tf_op jit(solution)/shard_map/all_to_all | solution.py:210
  260.4 69.5 %reduce-scatter.2.cloned.1.call-done = bf16[64,29,512]{2,1,0:T(8,128)(2,1)} async-done(((bf16[256,29,512]{2,1,0:T(8,128)(2,1)}), bf16[64,29,512]{2,1,0:T(8,128)(2,1)}) %reduce-scatter.2.cloned.1.call-update) | async-done | bytes 1900560 | tf_op jit(solution)/shard_map/reduce_scatter | solution.py:253
  330.0 2.7 multiply_convert_fusion
  337.0 0.9 convolution_convert_fusion.2
  338.2 0.7 copy.67
  (552 shorter events, 20.1 us)
Async XLA Ops:
  6.5 215.9 %copy-start = (bf16[7,64,7,256]{3,1,2,0:T(8,128)(2,1)S(1)}, bf16[7,64,7,256]{3,1,2,0:T(8,128)(2,1)}, u32[]{:S(2)}) copy-start(bf16[7,64,7,256]{3,1,2,0:T(8,128)(2,1)} %param.47) | copy-start | bytes 4816900
  14.2 22.7 %all-to-all-start = ((s32[64,1,16]{2,1,0:T(1,128)}), s32[64,1,16]{2,1,0:T(1,128)S(1)}, u32[]{:S(2)}, u32[]{:S(2)}) async-start(s32[64,1,16]{2,1,0:T(1,128)} %bitcast.27), calls=%async_computation | async-start | bytes 65536 | tf_op jit(solution)/shard_map/all_to_all | solution.py:240
  52.1 150.4 %all-to-all-start.1 = ((bf16[64,16,3136]{2,1,0:T(8,128)(2,1)}), bf16[64,16,3136]{2,1,0:T(8,128)(2,1)}, u32[]{:S(2)}, u32[]{:S(2)}) async-start(bf16[64,16,3136]{2,1,0:T(8,128)(2,1)} %bitcast.1284), calls=%async_computation.1 | async-start | bytes 13107200 | tf_op jit(solution)/shard_map/all_to_all | solution.py:242
  57.9 272.0 %reduce-scatter.2.cloned.1.call-start = ((), (), s32[]{:S(2)}) async-start(), calls=%async_computation.4 | async-start | bytes 10485760 | tf_op jit(solution)/shard_map/reduce_scatter | solution.py:253
  62.0 24.0 %copy-start.3 = (bf16[2,5,64,5,256]{4,2,3,1,0:T(8,128)(2,1)S(1)}, bf16[2,5,64,5,256]{4,2,3,1,0:T(8,128)(2,1)}, u32[]{:S(2)}) copy-start(bf16[2,5,64,5,256]{4,2,3,1,0:T(8,128)(2,1)} %param.49) | copy-start | bytes 4915204
  68.3 19.0 %copy-start.2 = (bf16[2,6,64,6,256]{4,2,3,1,0:T(8,128)(2,1)S(1)}, bf16[2,6,64,6,256]{4,2,3,1,0:T(8,128)(2,1)}, u32[]{:S(2)}) copy-start(bf16[2,6,64,6,256]{4,2,3,1,0:T(8,128)(2,1)} %param.48) | copy-start | bytes 7077892
  202.6 9.2 %copy-start.159 = (f32[1,512]{1,0:T(1,128)S(1)}, f32[1,512]{1,0:T(1,128)}, u32[]{:S(2)}) copy-start(f32[1,512]{1,0:T(1,128)} %get-tuple-element.196) | copy-start | bytes 6148
  202.6 9.2 %copy-start.167 = (f32[1,512]{1,0:T(1,128)S(1)}, f32[1,512]{1,0:T(1,128)}, u32[]{:S(2)}) copy-start(f32[1,512]{1,0:T(1,128)} %get-tuple-element.197) | copy-start | bytes 6148
  202.6 9.2 %copy-start.172 = (f32[1,512]{1,0:T(1,128)S(1)}, f32[1,512]{1,0:T(1,128)}, u32[]{:S(2)}) copy-start(f32[1,512]{1,0:T(1,128)} %get-tuple-element.198) | copy-start | bytes 6148
  202.6 10.0 %copy-start.93 = (f32[1,512]{1,0:T(1,128)S(1)}, f32[1,512]{1,0:T(1,128)}, u32[]{:S(2)}) copy-start(f32[1,512]{1,0:T(1,128)} %get-tuple-element.187) | copy-start | bytes 6148
  202.6 10.0 %copy-start.103 = (f32[1,512]{1,0:T(1,128)S(1)}, f32[1,512]{1,0:T(1,128)}, u32[]{:S(2)}) copy-start(f32[1,512]{1,0:T(1,128)} %get-tuple-element.188) | copy-start | bytes 6148
  202.6 10.0 %copy-start.110 = (f32[1,512]{1,0:T(1,128)S(1)}, f32[1,512]{1,0:T(1,128)}, u32[]{:S(2)}) copy-start(f32[1,512]{1,0:T(1,128)} %get-tuple-element.190) | copy-start | bytes 6148
  202.7 10.0 %copy-start.116 = (f32[1,512]{1,0:T(1,128)S(1)}, f32[1,512]{1,0:T(1,128)}, u32[]{:S(2)}) copy-start(f32[1,512]{1,0:T(1,128)} %get-tuple-element.191) | copy-start | bytes 6148
  202.7 10.0 %copy-start.121 = (f32[1,512]{1,0:T(1,128)S(1)}, f32[1,512]{1,0:T(1,128)}, u32[]{:S(2)}) copy-start(f32[1,512]{1,0:T(1,128)} %get-tuple-element.192) | copy-start | bytes 6148
  202.7 10.0 %copy-start.127 = (f32[1,512]{1,0:T(1,128)S(1)}, f32[1,512]{1,0:T(1,128)}, u32[]{:S(2)}) copy-start(f32[1,512]{1,0:T(1,128)} %get-tuple-element.193) | copy-start | bytes 6148
  202.7 10.0 %copy-start.135 = (f32[1,512]{1,0:T(1,128)S(1)}, f32[1,512]{1,0:T(1,128)}, u32[]{:S(2)}) copy-start(f32[1,512]{1,0:T(1,128)} %get-tuple-element.194) | copy-start | bytes 6148
  202.7 10.0 %copy-start.141 = (f32[1,512]{1,0:T(1,128)S(1)}, f32[1,512]{1,0:T(1,128)}, u32[]{:S(2)}) copy-start(f32[1,512]{1,0:T(1,128)} %get-tuple-element.195) | copy-start | bytes 6148
  202.7 10.0 %copy-start.149 = (f32[1,512]{1,0:T(1,128)S(1)}, f32[1,512]{1,0:T(1,128)}, u32[]{:S(2)}) copy-start(f32[1,512]{1,0:T(1,128)} %get-tuple-element.189) | copy-start | bytes 6148
  202.7 10.1 %copy-start.12 = (f32[1,512]{1,0:T(1,128)S(1)}, f32[1,512]{1,0:T(1,128)}, u32[]{:S(2)}) copy-start(f32[1,512]{1,0:T(1,128)} %get-tuple-element.176) | copy-start | bytes 6148
  202.7 10.1 %copy-start.18 = (f32[1,512]{1,0:T(1,128)S(1)}, f32[1,512]{1,0:T(1,128)}, u32[]{:S(2)}) copy-start(f32[1,512]{1,0:T(1,128)} %get-tuple-element.177) | copy-start | bytes 6148
  202.7 10.1 %copy-start.25 = (f32[1,512]{1,0:T(1,128)S(1)}, f32[1,512]{1,0:T(1,128)}, u32[]{:S(2)}) copy-start(f32[1,512]{1,0:T(1,128)} %get-tuple-element.178) | copy-start | bytes 6148
  202.7 10.1 %copy-start.31 = (f32[1,512]{1,0:T(1,128)S(1)}, f32[1,512]{1,0:T(1,128)}, u32[]{:S(2)}) copy-start(f32[1,512]{1,0:T(1,128)} %get-tuple-element.179) | copy-start | bytes 6148
  202.8 10.1 %copy-start.37 = (f32[1,512]{1,0:T(1,128)S(1)}, f32[1,512]{1,0:T(1,128)}, u32[]{:S(2)}) copy-start(f32[1,512]{1,0:T(1,128)} %get-tuple-element.180) | copy-start | bytes 6148
  202.8 10.1 %copy-start.43 = (f32[1,512]{1,0:T(1,128)S(1)}, f32[1,512]{1,0:T(1,128)}, u32[]{:S(2)}) copy-start(f32[1,512]{1,0:T(1,128)} %get-tuple-element.181) | copy-start | bytes 6148
  202.8 10.1 %copy-start.49 = (f32[1,512]{1,0:T(1,128)S(1)}, f32[1,512]{1,0:T(1,128)}, u32[]{:S(2)}) copy-start(f32[1,512]{1,0:T(1,128)} %get-tuple-element.182) | copy-start | bytes 6148
  202.8 10.1 %copy-start.56 = (f32[1,512]{1,0:T(1,128)S(1)}, f32[1,512]{1,0:T(1,128)}, u32[]{:S(2)}) copy-start(f32[1,512]{1,0:T(1,128)} %get-tuple-element.183) | copy-start | bytes 6148
  202.8 10.1 %copy-start.63 = (f32[1,512]{1,0:T(1,128)S(1)}, f32[1,512]{1,0:T(1,128)}, u32[]{:S(2)}) copy-start(f32[1,512]{1,0:T(1,128)} %get-tuple-element.184) | copy-start | bytes 6148
  202.8 10.1 %copy-start.71 = (f32[1,512]{1,0:T(1,128)S(1)}, f32[1,512]{1,0:T(1,128)}, u32[]{:S(2)}) copy-start(f32[1,512]{1,0:T(1,128)} %get-tuple-element.185) | copy-start | bytes 6148
  202.8 10.1 %copy-start.82 = (f32[1,512]{1,0:T(1,128)S(1)}, f32[1,512]{1,0:T(1,128)}, u32[]{:S(2)}) copy-start(f32[1,512]{1,0:T(1,128)} %get-tuple-element.186) | copy-start | bytes 6148
  247.7 85.1 %copy-start.164 = (f32[1,512]{1,0:T(1,128)S(1)}, f32[1,512]{1,0:T(1,128)}, u32[]{:S(2)}) copy-start(f32[1,512]{1,0:T(1,128)} %get-tuple-element.162) | copy-start | bytes 6148
  247.7 85.1 %copy-start.201 = (f32[1,512]{1,0:T(1,128)S(1)}, f32[1,512]{1,0:T(1,128)}, u32[]{:S(2)}) copy-start(f32[1,512]{1,0:T(1,128)} %get-tuple-element.208) | copy-start | bytes 6148
  247.7 85.2 %copy-start.158 = (f32[1,512]{1,0:T(1,128)S(1)}, f32[1,512]{1,0:T(1,128)}, u32[]{:S(2)}) copy-start(f32[1,512]{1,0:T(1,128)} %get-tuple-element.161) | copy-start | bytes 6148
  247.7 85.2 %copy-start.199 = (f32[1,512]{1,0:T(1,128)S(1)}, f32[1,512]{1,0:T(1,128)}, u32[]{:S(2)}) copy-start(f32[1,512]{1,0:T(1,128)} %get-tuple-element.210) | copy-start | bytes 6148
  247.7 85.2 %copy-start.152 = (f32[1,512]{1,0:T(1,128)S(1)}, f32[1,512]{1,0:T(1,128)}, u32[]{:S(2)}) copy-start(f32[1,512]{1,0:T(1,128)} %get-tuple-element.160) | copy-start | bytes 6148
  247.8 85.2 %copy-start.198 = (f32[1,512]{1,0:T(1,128)S(1)}, f32[1,512]{1,0:T(1,128)}, u32[]{:S(2)}) copy-start(f32[1,512]{1,0:T(1,128)} %get-tuple-element.209) | copy-start | bytes 6148
  247.8 85.3 %copy-start.144 = (f32[1,512]{1,0:T(1,128)S(1)}, f32[1,512]{1,0:T(1,128)}, u32[]{:S(2)}) copy-start(f32[1,512]{1,0:T(1,128)} %get-tuple-element.159) | copy-start | bytes 6148
  247.8 85.3 %copy-start.202 = (f32[1,512]{1,0:T(1,128)S(1)}, f32[1,512]{1,0:T(1,128)}, u32[]{:S(2)}) copy-start(f32[1,512]{1,0:T(1,128)} %get-tuple-element.207) | copy-start | bytes 6148
  247.8 85.4 %copy-start.134 = (f32[1,512]{1,0:T(1,128)S(1)}, f32[1,512]{1,0:T(1,128)}, u32[]{:S(2)}) copy-start(f32[1,512]{1,0:T(1,128)} %get-tuple-element.158) | copy-start | bytes 6148
  247.8 85.4 %copy-start.200 = (f32[1,512]{1,0:T(1,128)S(1)}, f32[1,512]{1,0:T(1,128)}, u32[]{:S(2)}) copy-start(f32[1,512]{1,0:T(1,128)} %get-tuple-element.206) | copy-start | bytes 6148
  247.8 85.5 %copy-start.126 = (f32[1,512]{1,0:T(1,128)S(1)}, f32[1,512]{1,0:T(1,128)}, u32[]{:S(2)}) copy-start(f32[1,512]{1,0:T(1,128)} %get-tuple-element.157) | copy-start | bytes 6148
  247.8 85.5 %copy-start.197 = (f32[1,512]{1,0:T(1,128)S(1)}, f32[1,512]{1,0:T(1,128)}, u32[]{:S(2)}) copy-start(f32[1,512]{1,0:T(1,128)} %get-tuple-element.205) | copy-start | bytes 6148
  247.8 85.6 %copy-start.196 = (f32[1,512]{1,0:T(1,128)S(1)}, f32[1,512]{1,0:T(1,128)}, u32[]{:S(2)}) copy-start(f32[1,512]{1,0:T(1,128)} %get-tuple-element.204) | copy-start | bytes 6148
  248.9 11.5 %all-to-all-start.2 = ((bf16[4,1,128]{2,1,0:T(2,128)(2,1)}), bf16[4,1,128]{2,1,0:T(2,128)(2,1)S(1)}, u32[]{:S(2)}, u32[]{:S(2)}) async-start(bf16[4,1,128]{2,1,0:T(2,128)(2,1)} %stack.36), calls=%async_computation.3 | async-start | bytes 4096 | tf_op jit(solution)/shard_map/all_to_all | solution.py:210
  260.4 73.2 %copy-start.193 = (f32[1,512]{1,0:T(1,128)S(1)}, f32[1,512]{1,0:T(1,128)}, u32[]{:S(2)}) copy-start(f32[1,512]{1,0:T(1,128)} %get-tuple-element.203) | copy-start | bytes 6148
  260.4 73.3 %copy-start.190 = (f32[1,512]{1,0:T(1,128)S(1)}, f32[1,512]{1,0:T(1,128)}, u32[]{:S(2)}) copy-start(f32[1,512]{1,0:T(1,128)} %get-tuple-element.202) | copy-start | bytes 6148
  260.4 73.4 %copy-start.187 = (f32[1,512]{1,0:T(1,128)S(1)}, f32[1,512]{1,0:T(1,128)}, u32[]{:S(2)}) copy-start(f32[1,512]{1,0:T(1,128)} %get-tuple-element.201) | copy-start | bytes 6148
  260.4 73.4 %copy-start.183 = (f32[1,512]{1,0:T(1,128)S(1)}, f32[1,512]{1,0:T(1,128)}, u32[]{:S(2)}) copy-start(f32[1,512]{1,0:T(1,128)} %get-tuple-element.200) | copy-start | bytes 6148
  260.4 73.5 %copy-start.178 = (f32[1,512]{1,0:T(1,128)S(1)}, f32[1,512]{1,0:T(1,128)}, u32[]{:S(2)}) copy-start(f32[1,512]{1,0:T(1,128)} %get-tuple-element.199) | copy-start | bytes 6148
  (166 other events, 394.7 us)
Sparse Core Ops, SparseCore 0:
  247.8 82.0 reduce-scatter.1
